TPU v7x, 32 devices: a whole 2x2x4 slice. The times are simulated.
32 devices in a mesh: grp: 2 (over x), gx: 16 (over z, y, core).
Axes of the slice: x: 2, y: 2, z: 4, core: 2. Of those that a mesh axis runs over, the one named last changes fastest.
Arguments:
- remaining_states: bfloat16 [128, 16384], P(('grp', 'gx')), parts along dimension 0, may hold values from -6 to 6
- scaling_factor_vector: bfloat16 [16384], replicated, may hold values from 0.25 to 1.75
- probe_projection_matrix: bfloat16 [16384, 8192], P(None, 'gx'), may hold values from -1 to 1
- memory_projection_matrix: bfloat16 [16384, 1024], P('gx'), may hold values from -0.046875 to 0.046875
- final_projection_matrix: bfloat16 [8192, 16384], P('gx'), may hold values from -0.0625 to 0.0625
- memorized_address_tensor: bfloat16 [1024, 128, 512], P(('grp', 'gx')), parts along dimension 0, may hold values from -8 to 8
- memorized_content_tensor: bfloat16 [1024, 128, 512], P(('grp', 'gx')), parts along dimension 0, may hold values from -6 to 6
- retained_sequence_ids: int32 [128], P('grp'), parts along dimension 0, may hold values from 0 to 511, as said below
- occupied_positions: int32 [1024], P(('grp', 'gx')), parts along dimension 0, may hold values from 1 to 128
Outputs:
- result: bfloat16 [128, 16384], P(('grp', 'gx')), parts along dimension 0
There are 2 independent parts, one for each index of `grp`. A program takes and returns all parts, laid end to end along the dimension named above; an argument that names none is the same for every part. Nothing has to cross between parts.
Inputs may be any that keep to these rules, and one draw needn't show every extreme that they name: Distinct batch rows; row r of remaining_states belongs to batch row retained_sequence_ids[r].
All inputs are finite; a program needn't handle non-finite values.
Results may differ from a plain program's by a relative error of at most 0.014.
Values may be sent and summed in bfloat16 or wider, within the bound.
A program may use at most 192 MiB of HBM per device.

v0:
```python
import jax
import jax.numpy as jnp
from jax import lax
from jax.sharding import PartitionSpec as P

HEADS = 64
KV = 4
DH = 128
CACHE = 128


epsilon = 1e-05


def normalize(remaining_states, scaling_factor_vector):
    values = remaining_states.astype(jnp.float32)
    inverse = lax.rsqrt(jnp.mean(values * values, axis=1, keepdims=True) + epsilon)
    return (values * inverse * scaling_factor_vector.astype(jnp.float32)).astype(jnp.bfloat16)


def attend_slots(probe_vectors, new_kv, keys, values, slot_lengths):
    slots = probe_vectors.shape[0]
    query_heads = probe_vectors.reshape(slots, KV, HEADS // KV, DH)
    key_heads = keys.reshape(slots, CACHE, KV, DH)
    value_heads = values.reshape(slots, CACHE, KV, DH)
    inverse = 1.0 / jnp.sqrt(jnp.float32(DH))
    scores = (
        jnp.einsum("skgd,sjkd->skgj", query_heads, key_heads, preferred_element_type=jnp.float32)
        * inverse
    )
    visible = (jnp.arange(CACHE, dtype=jnp.int32)[None, :] < slot_lengths[:, None])[
        :, None, None, :
    ]
    scores = jnp.where(visible, scores, jnp.float32(-1e30))
    new_keys = new_kv[:, : KV * DH].astype(jnp.float32).reshape(slots, KV, 1, DH)
    new_values = new_kv[:, KV * DH :].astype(jnp.float32).reshape(slots, KV, 1, DH)
    own_score = jnp.sum(query_heads.astype(jnp.float32) * new_keys, axis=-1) * inverse
    highest = jnp.maximum(jnp.max(scores, axis=-1), own_score)
    expo_cache = jnp.where(visible, jnp.exp(scores - highest[..., None]), jnp.float32(0.0))
    expo_new = jnp.exp(own_score - highest)
    denominator = jnp.sum(expo_cache, axis=-1) + expo_new
    weights = (expo_cache / denominator[..., None]).astype(jnp.bfloat16)
    weight_new = (expo_new / denominator).astype(jnp.bfloat16)
    summed = jnp.einsum("skgj,sjkd->skgd", weights, value_heads, preferred_element_type=jnp.float32)
    summed = summed + weight_new.astype(jnp.float32)[..., None] * new_values
    return summed.reshape(slots, HEADS * DH).astype(jnp.bfloat16)


def local(
    remaining_states,
    scaling_factor_vector,
    probe_projection_matrix,
    memory_projection_matrix,
    final_projection_matrix,
    memorized_address_tensor,
    memorized_content_tensor,
    retained_sequence_ids,
    occupied_positions,
):
    group_size = lax.axis_size("gx")
    local_ordinal = lax.axis_index("gx")
    sequence_count_local = memorized_address_tensor.shape[0]
    complete_sequence_set = sequence_count_local * group_size
    retained_ordinal = (
        retained_sequence_ids[:, None]
        == jnp.arange(complete_sequence_set, dtype=jnp.int32)[None, :]
    ).astype(jnp.bfloat16)
    normed_all = lax.all_gather(
        normalize(remaining_states, scaling_factor_vector), "gx", axis=0, tiled=True
    )
    probe_vectors = jnp.dot(
        normed_all, probe_projection_matrix, preferred_element_type=jnp.float32
    ).astype(jnp.bfloat16)
    width_dev = memory_projection_matrix.shape[0]
    normed_cols = lax.dynamic_slice_in_dim(normed_all, local_ordinal * width_dev, width_dev, 1)
    kv_part = jnp.dot(normed_cols, memory_projection_matrix, preferred_element_type=jnp.float32)
    slot_select = jnp.transpose(retained_ordinal).astype(jnp.float32)
    sliced = slot_select
    new_kv = lax.psum_scatter(
        jnp.dot(sliced, kv_part, precision=lax.Precision.HIGHEST),
        "gx",
        scatter_dimension=0,
        tiled=True,
    ).astype(jnp.bfloat16)
    query_slots = jnp.einsum(
        "wa,wy->ay", retained_ordinal, probe_vectors, preferred_element_type=jnp.float32
    ).astype(jnp.bfloat16)
    owner_queries = lax.all_to_all(query_slots, "gx", split_axis=0, concat_axis=1, tiled=True)
    attended = attend_slots(
        owner_queries,
        new_kv,
        memorized_address_tensor,
        memorized_content_tensor,
        occupied_positions,
    )
    final_result = lax.all_to_all(attended, "gx", split_axis=1, concat_axis=0, tiled=True)
    contextual_states = jnp.dot(
        retained_ordinal, final_result, preferred_element_type=jnp.float32
    ).astype(jnp.bfloat16)
    sliced = contextual_states
    projected = lax.psum_scatter(
        jnp.dot(sliced, final_projection_matrix, preferred_element_type=jnp.float32),
        "gx",
        scatter_dimension=0,
        tiled=True,
    )
    return (remaining_states.astype(jnp.float32) + projected).astype(jnp.bfloat16)


def solution(mesh):
    placed = (
        P(("grp", "gx"), None),
        P(),
        P(None, "gx"),
        P("gx", None),
        P("gx", None),
        P(("grp", "gx"), None, None),
        P(("grp", "gx"), None, None),
        P("grp"),
        P(("grp", "gx")),
    )
    return jax.shard_map(
        local, mesh=mesh, in_specs=placed, out_specs=P(("grp", "gx"), None), check_vma=False
    )
```

profile of v0, /device:TPU:0, one launch (start us, length us, event | category | flops | bytes accessed | tf_op | source)
XLA Modules:
  0.0 279.0 jit_solution(12544201590085634348)
XLA Ops:
  6.5 0.0 copy-start
  6.5 0.0 copy-start.2
  6.5 0.0 all-gather.3.cloned.1.call-start
  6.5 0.9 convert_element_type.57
  7.5 1.2 fusion.24
  8.6 1.7 fusion.28
  10.3 0.0 all-gather.3.cloned.1.call-update
  10.3 0.0 reduce-scatter.2.cloned.1.call-start
  10.4 44.3 %all-gather.3.cloned.1.call-done = bf16[16,4,16384]{2,1,0:T(4,128)(2,1)} async-done(((bf16[1,4,16384]{2,1,0:T(4,128)(2,1)}), bf16[16,4,16384]{2,1,0:T(4,128)(2,1)}) %all-gather.3.cloned.1.call-update) | async-done | bytes 2097168 | tf_op jit(solution)/shard_map/all_gather | solution.py:68
  54.7 4.0 %reshape.80 = bf16[64,16384]{1,0:T(8,128)(2,1)} reshape(bf16[16,4,16384]{2,1,0:T(4,128)(2,1)} %all-gather.3.cloned.1.call-done) | data formatting | bytes 4194304
  58.6 0.0 copy-done
  58.6 1.4 fusion.29
  60.0 0.0 copy-done.2
  60.0 2.4 fusion.31
  62.5 0.0 reduce-scatter.2.cloned.1.call-update
  62.5 0.0 copy-start.3
  62.5 10.7 %convolution_convert_fusion = bf16[512,512]{1,0:T(8,128)(2,1)} fusion(bf16[64,16384]{1,0:T(8,128)(2,1)} %reshape.80, bf16[16384,512]{1,0:T(8,128)(2,1)} %param.11, s32[64]{0:T(128)S(1)} %copy-done.2), kind=kOutput, calls=%fused_computation.10 | convolution fusion | flops 1107623936 | bytes 19398912 | tf_op jit(solution)/shard_map/wa,wy->ay/dot_general | solution.py:85
  73.2 3.6 %all-to-all-start = ((bf16[16,32,512]{2,1,0:T(8,128)(2,1)}), bf16[16,32,512]{2,1,0:T(8,128)(2,1)S(1)}, u32[]{:S(2)}, u32[]{:S(2)}) async-start(bf16[16,32,512]{2,1,0:T(8,128)(2,1)} %bitcast.1), calls=%async_computation | async-start | bytes 1048576 | tf_op jit(solution)/shard_map/all_to_all | solution.py:88
  76.8 0.0 all-reduce.3.cloned.1.call-start
  76.8 0.0 copy-done.3
  76.8 0.1 iota_compare_fusion.5
  76.9 14.1 %all-to-all-done = bf16[16,32,512]{2,1,0:T(8,128)(2,1)S(1)} async-done(((bf16[16,32,512]{2,1,0:T(8,128)(2,1)}), bf16[16,32,512]{2,1,0:T(8,128)(2,1)S(1)}, u32[]{:S(2)}, u32[]{:S(2)}) %all-to-all-start) | async-done | bytes 524320 | tf_op jit(solution)/shard_map/all_to_all | solution.py:88
  91.0 0.3 copy.17
  91.3 0.3 reshape.74
  91.6 5.5 %fusion.40 = (f32[32,4,16]{2,1,0:T(4,128)S(1)}, f32[32,4,16,128]{3,2,1,0:T(8,128)}) fusion(bf16[32,4,16,128]{3,2,1,0:T(8,128)(2,1)S(1)} %reshape.74, pred[32,128]{1,0:T(8,128)(4,1)S(1)} %iota_compare_fusion.5, bf16[32,128,512]{2,1,0:T(8,128)(2,1)} %param.14), kind=kOutput, calls=%fused_computation.48 | convolution fusion | flops 67893248 | bytes 5779456 | tf_op jit(solution)/shard_map/skgd,sjkd->skgj/dot_general | solution.py:28
  97.1 26.1 %reduce-scatter.2.cloned.1.call-done = f32[32,1024]{1,0:T(8,128)} async-done(((f32[512,1024]{1,0:T(8,128)}), f32[32,1024]{1,0:T(8,128)}) %reduce-scatter.2.cloned.1.call-update) | async-done | bytes 131088 | tf_op jit(solution)/shard_map/reduce_scatter | solution.py:79
  123.2 0.9 convert_element_type.62
  124.2 0.4 multiply_reduce_fusion
  124.6 1.9 fusion.19
  126.5 0.1 fusion.37
  126.6 3.8 %fusion.15 = bf16[32,4,16,128]{3,2,1,0:T(8,128)(2,1)S(1)} fusion(f32[32,4,16,128]{3,2,1,0:T(8,128)} %get-tuple-element.10, f32[32,4,128]{2,1,0:T(4,128)S(1)} %reshape.78, f32[32,4,16]{2,1,0:T(4,128)S(1)} %get-tuple-element.6, f32[32,4,16]{2,1,0:T(4,128)S(1)} %get-tuple-element.5, f32[32,4,16]{2,1,0:T(4,128)S(1)} %multiply_maximum_fusion, ...), kind=kOutput, calls=%fused_computation.9 | convolution fusion | flops 68943872 | bytes 5861376 | tf_op jit(solution)/shard_map/skgj,sjkd->skgd/dot_general | solution.py:44
  130.4 0.3 convert_element_type.67
  130.7 0.3 copy.20
  131.0 17.7 %all_to_all.32 = bf16[32,16,512]{2,0,1:T(8,128)(2,1)S(1)} all-to-all(bf16[32,16,512]{2,0,1:T(8,128)(2,1)S(1)} %copy.20), channel_id=1, replica_groups=mesh['grp'=2,'gx'=16] {'gx'}, dimensions={1} | all-to-all | bytes 1048576 | tf_op jit(solution)/shard_map/all_to_all | solution.py:96
  148.7 11.0 %fusion.18 = f32[64,16384]{1,0:T(8,128)} fusion(bf16[512,16384]{1,0:T(8,128)(2,1)} %param.13, bf16[512,512]{1,0:T(8,128)(2,1)S(1)} %bitcast.41, s32[64]{0:T(128)S(1)} %copy-done.2), kind=kOutput, calls=%fused_computation.13 | convolution fusion | flops 1107361792 | bytes 21496064 | tf_op jit(solution)/shard_map/dot_general | solution.py:102
  159.7 0.0 copy-start.4
  159.7 0.0 copy-start.1
  159.7 0.0 all-reduce.3.cloned.1.call-update
  159.7 0.6 copy-done.4
  160.4 0.6 dynamic-slice
  161.6 109.1 %all-reduce.3.cloned.1.call-done = f32[64,16384]{1,0:T(8,128)} async-done(((f32[64,16384]{1,0:T(8,128)}), f32[64,16384]{1,0:T(8,128)}) %all-reduce.3.cloned.1.call-update) | async-done | bytes 4194320
  270.7 0.0 copy-done.1
  270.7 1.8 fusion.27
  (5 shorter events, 0.1 us)
Async XLA Ops:
  6.5 52.1 %copy-start = (bf16[1024,1024]{1,0:T(8,128)(2,1)S(1)}, bf16[1024,1024]{1,0:T(8,128)(2,1)}, u32[]{:S(2)}) copy-start(bf16[1024,1024]{1,0:T(8,128)(2,1)} %param.12) | copy-start | bytes 6291460
  6.5 53.5 %copy-start.2 = (s32[64]{0:T(128)S(1)}, s32[64]{0:T(128)}, u32[]{:S(2)}) copy-start(s32[64]{0:T(128)} %param.16) | copy-start | bytes 772
  6.5 48.1 %all-gather.3.cloned.1.call-start = ((), (), s32[]{:S(2)}) async-start(), calls=%async_computation.4 | async-start | bytes 2228224 | tf_op jit(solution)/shard_map/all_gather | solution.py:68
  10.3 112.9 %reduce-scatter.2.cloned.1.call-start = ((), (), s32[]{:S(2)}) async-start(), calls=%async_computation.3 | async-start | bytes 2228224 | tf_op jit(solution)/shard_map/reduce_scatter | solution.py:79
  62.5 14.3 %copy-start.3 = (s32[32]{0:T(128)S(1)}, s32[32]{0:T(128)}, u32[]{:S(2)}) copy-start(s32[32]{0:T(128)} %param.17) | copy-start | bytes 388
  73.2 17.8 %all-to-all-start = ((bf16[16,32,512]{2,1,0:T(8,128)(2,1)}), bf16[16,32,512]{2,1,0:T(8,128)(2,1)S(1)}, u32[]{:S(2)}, u32[]{:S(2)}) async-start(bf16[16,32,512]{2,1,0:T(8,128)(2,1)} %bitcast.1), calls=%async_computation | async-start | bytes 1048576 | tf_op jit(solution)/shard_map/all_to_all | solution.py:88
  76.8 193.9 %all-reduce.3.cloned.1.call-start = ((), (), s32[]{:S(2)}) async-start(), calls=%async_computation.5 | async-start | bytes 8388608
  159.7 0.7 copy-start.4
  159.7 111.0 %copy-start.1 = (bf16[4,16384]{1,0:T(4,128)(2,1)S(1)}, bf16[4,16384]{1,0:T(4,128)(2,1)}, u32[]{:S(2)}) copy-start(bf16[4,16384]{1,0:T(4,128)(2,1)} %param.9) | copy-start | bytes 393220
Sparse Core Ops, SparseCore 0:
  10.5 44.1 all-gather.2
  62.6 60.5 reduce-scatter.1
  159.9 110.7 all-reduce.2
where the time goes:
time: 280 us; the launch traced here: 279 us
  waiting for transfers between devices  194 us (69%)
  matrix products  34.8 us (12%)
  blocking collectives  17.7 us (6%)
  between operations  13.9 us (5%)
  other arithmetic  8.92 us (3%)
  local copies, waits for them, and re-layouts  6.45 us (2%)
  starting transfers between devices  3.66 us (1%)
    unnamed x4, waiting for transfers between devices  109 us
    all_gather x1, waiting for transfers between devices, local(): lax.all_gather(normalize(remaining_states, scaling_factor_vector), 'gx',...  44.3 us
    reduce_scatter x1, waiting for transfers between devices, local(): lax.psum_scatter(jnp.dot(sliced, kv_part, precision=lax.Precision.HIGHEST...  26.1 us
    all_to_all x1, blocking collectives, local(): lax.all_to_all(attended, 'gx', split_axis=1, concat_axis=0, tiled=True)  17.7 us
    all_to_all x1, waiting for transfers between devices, local(): lax.all_to_all(query_slots, 'gx', split_axis=0, concat_axis=1, tiled=True)  14.1 us
    dot_general x1, matrix products, local(): jnp.dot(sliced, final_projection_matrix, preferred_element_type=jnp.float32)  11 us
    dot_general x1, matrix products, local(): jnp.einsum('wa,wy->ay', retained_ordinal, probe_vectors, preferred_elemen...  10.7 us
  transfers between devices with their start and end apart: 4, of which 4 were waited for; matrix products, arithmetic and copies ran while one was open for 6% of the time, Pallas kernels for 0%

commit v1 on v0

v1 whole, which is shorter than its diff:
```python
import functools
import jax
import jax.numpy as jnp
from jax import lax
from jax.experimental import pallas as pl
from jax.experimental.pallas import tpu as pltpu
from jax.sharding import PartitionSpec as P

HEADS = 64
KV = 4
DH = 128
CACHE = 128

epsilon = 1e-05
F32 = jnp.float32
BF16 = jnp.bfloat16


def place(n):
    me = lax.axis_index("gx")
    return me, me // 4, (me // 2) % 2, me % 2, n // 4


def dev(z, y, c):
    return (z * 2 + y) * 2 + c


def enter(n):
    me = lax.axis_index("gx")
    barrier = pltpu.get_barrier_semaphore()
    for k in range(1, n):
        pl.semaphore_signal(
            barrier,
            inc=1,
            device_id={"gx": lax.rem(me + k, n)},
            device_id_type=pl.DeviceIdType.MESH,
        )
    pl.semaphore_wait(barrier, n - 1)


def remote(src, dst, send, recv, target):
    return pltpu.make_async_remote_copy(
        src_ref=src,
        dst_ref=dst,
        send_sem=send,
        recv_sem=recv,
        device_id={"gx": target},
        device_id_type=pl.DeviceIdType.MESH,
    )


class Gather:
    def __init__(self, n, g, send, recv):
        self.n, self.g, self.send, self.recv = n, g, send, recv
        self.me, self.z, self.y, self.c, self.Z = place(n)
        self.other_y = dev(self.z, 1 - self.y, self.c)
        self.other_c = dev(self.z, self.y, 1 - self.c)

    def copy(self, ch, block, kind, target):
        return remote(
            self.g.at[ch, block],
            self.g.at[ch, block],
            self.send.at[kind, ch, block],
            self.recv.at[ch, block],
            target,
        )

    def arrived(self, ch, block):
        self.copy(ch, block, 3, self.other_c).wait_recv()

    def fan(self, ch, sz):
        block = dev(sz, self.y, self.c)
        z, Z = self.z, self.Z

        @pl.when((sz <= z) & (z < Z - 1))
        def _():
            self.copy(ch, block, 0, self.me + 4).start()

        @pl.when((sz >= z) & (z > 0))
        def _():
            self.copy(ch, block, 1, self.me - 4).start()

        self.copy(ch, block, 2, self.other_y).start()
        self.copy(ch, block, 3, self.other_c).start()

    def both(self, t, f):
        z, Z = self.z, self.Z
        if t == 0:
            f(z)
            return

        @pl.when(z >= t)
        def _():
            f(z - t)

        @pl.when(z + t < Z)
        def _():
            f(z + t)

    def own(self, ch):
        self.fan(ch, self.z)

    def line(self, ch, t):
        def f(sz):
            self.arrived(ch, dev(sz, self.y, self.c))
            self.fan(ch, sz)

        self.both(t, f)

    def across(self, ch, t):
        def f(sz):
            block = dev(sz, 1 - self.y, self.c)
            self.arrived(ch, block)
            self.copy(ch, block, 3, self.other_c).start()

        self.both(t, f)

    def rest(self, ch):
        for sz in range(self.Z):
            for y in range(2):
                self.arrived(ch, dev(sz, y, 1 - self.c))

    def drain(self, ch):
        z, Z = self.z, self.Z
        for sz in range(Z):
            block = dev(sz, self.y, self.c)

            @pl.when((sz <= z) & (z < Z - 1))
            def _():
                self.copy(ch, block, 0, self.other_c).wait_send()

            @pl.when((sz >= z) & (z > 0))
            def _():
                self.copy(ch, block, 1, self.other_c).wait_send()

            self.copy(ch, block, 2, self.other_y).wait_send()
            self.copy(ch, block, 3, self.other_c).wait_send()
            self.copy(ch, dev(sz, 1 - self.y, self.c), 3, self.other_c).wait_send()


def first_kernel(
    n, NC, x_ref, gain_ref, wq_hbm, wkv_hbm, q_ref, kv_ref,
    g, xfull, acc, wq, wkv, kvs, kvr,
    wq_sem, wkv_sem, g_send, g_recv, q_send, q_recv, kv_send, kv_recv, ks, kr,
):
    me, z, y, c, Z = place(n)
    rl, D = x_ref.shape
    R = n * rl
    CW = D // NC
    weight_copies = []
    for ch in range(NC):
        rows = pl.ds(ch * CW, CW)
        cp = pltpu.make_async_copy(wq_hbm.at[rows], wq.at[rows], wq_sem.at[ch])
        cp.start()
        weight_copies.append(cp)
    kv_copy = pltpu.make_async_copy(wkv_hbm, wkv, wkv_sem)
    kv_copy.start()

    square = jnp.zeros((rl, 1), F32)
    for ch in range(NC):
        v = x_ref[:, ch * CW : (ch + 1) * CW].astype(F32)
        square = square + jnp.sum(v * v, axis=1, keepdims=True)
    inverse = lax.rsqrt(square / D + epsilon)
    for ch in range(NC):
        cols = slice(ch * CW, (ch + 1) * CW)
        v = x_ref[:, cols].astype(F32) * inverse * gain_ref[:, cols].astype(F32)
        g[ch, me] = v.astype(BF16)

    enter(n)
    ag = Gather(n, g, g_send, g_recv)
    for ch in range(NC):
        ag.own(ch)

    width = wkv.shape[0]

    def load(ch):
        step = min(512, CW)

        def body(i, carry):
            off = pl.multiple_of(i * step, step)
            pieces = [g[ch, b, :, pl.ds(off, step)].astype(F32) for b in range(n)]
            full = jnp.concatenate(pieces, axis=0).astype(BF16)
            xfull[:, pl.ds(pl.multiple_of(ch * CW + i * step, step), step)] = full
            return carry

        lax.fori_loop(0, CW // step, body, 0)

    def multiply(ch):
        weight_copies[ch].wait()
        step = min(1024, CW)

        def body(i, carry):
            rows = pl.ds(pl.multiple_of(ch * CW + i * step, step), step)
            acc[...] += jnp.dot(xfull[:, rows], wq[rows, :], preferred_element_type=F32)
            return carry

        lax.fori_loop(0, CW // step, body, 0)

    acc[...] = jnp.zeros_like(acc)
    LAG = 2
    for w in range(1, NC + Z + LAG + 1):
        for ch in range(NC):
            t = w - ch
            if 1 <= t < Z:
                ag.line(ch, t)
            ty = t - LAG
            if 0 <= ty < Z:
                ag.across(ch, ty)
            if ty == Z:
                ag.rest(ch)
                load(ch)
                if ch < NC - 1:
                    multiply(ch)

    kv_copy.wait()
    part = jnp.dot(
        xfull[:, pl.ds(pl.multiple_of(me * width, width), width)],
        wkv[...],
        preferred_element_type=F32,
    )
    for p in range(n):
        kvs[p] = part[p * rl : (p + 1) * rl].astype(BF16)
    for k in range(1, n):
        p = lax.rem(me + k, n)
        remote(kvs.at[p], kvr.at[me], ks.at[p], kr.at[me], p).start()
    multiply(NC - 1)

    q_ref[0, me] = acc[...].astype(BF16)
    qg = Gather(n, q_ref, q_send, q_recv)
    qg.own(0)
    total = kvs[me].astype(F32)
    for k in range(1, n):
        p = lax.rem(me + k, n)
        remote(kvs.at[p], kvr.at[p], ks.at[p], kr.at[p], p).wait_recv()
        total = total + kvr[p].astype(F32)
    kv_ref[0, me] = total.astype(BF16)
    kg = Gather(n, kv_ref, kv_send, kv_recv)
    kg.own(0)
    for w in range(1, Z + LAG + 1):
        if w < Z:
            qg.line(0, w)
            kg.line(0, w)
        if 0 <= w - LAG < Z:
            qg.across(0, w - LAG)
            kg.across(0, w - LAG)
    qg.rest(0)
    kg.rest(0)
    for ch in range(NC):
        ag.drain(ch)
    qg.drain(0)
    kg.drain(0)
    for k in range(1, n):
        p = lax.rem(me + k, n)
        remote(kvs.at[p], kvr.at[me], ks.at[p], kr.at[me], p).wait_send()


def project_in(n, x, gain, wq, wkv):
    rl, D = x.shape
    NC = 4
    CW = D // NC
    cols = wq.shape[1]
    wide = wkv.shape[1]
    R = n * rl
    vm = pl.BlockSpec(memory_space=pltpu.VMEM)
    hbm = pl.BlockSpec(memory_space=pl.ANY)
    dma = pltpu.SemaphoreType.DMA
    q, kv = pl.pallas_call(
        functools.partial(first_kernel, n, NC),
        out_shape=(
            jax.ShapeDtypeStruct((1, n, R, cols), BF16),
            jax.ShapeDtypeStruct((1, n, rl, wide), BF16),
        ),
        in_specs=[vm, vm, hbm, hbm],
        out_specs=(vm, vm),
        scratch_shapes=[
            pltpu.VMEM((NC, n, rl, CW), BF16),
            pltpu.VMEM((R, D), BF16),
            pltpu.VMEM((R, cols), F32),
            pltpu.VMEM((D, cols), BF16),
            pltpu.VMEM(wkv.shape, BF16),
            pltpu.VMEM((n, rl, wide), BF16),
            pltpu.VMEM((n, rl, wide), BF16),
            dma((NC,)),
            dma,
            dma((4, NC, n)),
            dma((NC, n)),
            dma((4, 1, n)),
            dma((1, n)),
            dma((4, 1, n)),
            dma((1, n)),
            dma((n,)),
            dma((n,)),
        ],
        compiler_params=pltpu.CompilerParams(
            collective_id=0, has_side_effects=True, vmem_limit_bytes=60 * 1024 * 1024
        ),
        name="project_in",
    )(x, gain.reshape(1, D), wq, wkv)
    return q[0], kv[0]


def second_kernel(
    n, NF, att_ref, ret_ref, x_ref, wo_hbm, out_ref,
    wo, ra, rows, pf, cs, cr, s1, ys, yr, zf, zs, zr,
    wo_sem, a_send, a_recv, c_send, c_recv, y_send, y_recv, z_send, z_recv,
):
    me, z, y, c, Z = place(n)
    rl, D = x_ref.shape
    R = n * rl
    NW = D // NF
    H, Q = R // 2, R // 4
    other_y, other_c = dev(z, 1 - y, c), dev(z, y, 1 - c)
    weight_copies = []
    for ch in range(NF):
        cols = pl.ds(ch * NW, NW)
        cp = pltpu.make_async_copy(wo_hbm.at[:, cols], wo.at[:, cols], wo_sem.at[ch])
        cp.start()
        weight_copies.append(cp)
    enter(n)
    for k in range(1, n):
        p = lax.rem(me + k, n)
        remote(att_ref.at[p], ra.at[me], a_send.at[p], a_recv.at[me], p).start()
    ra[me] = att_ref[me]
    for k in range(1, n):
        p = lax.rem(me + k, n)
        remote(att_ref.at[p], ra.at[p], a_send.at[p], a_recv.at[p], p).wait_recv()
    slots = ra.shape[0] * ra.shape[1]
    rows[...] = jnp.dot(
        ret_ref[...], ra[...].reshape(slots, ra.shape[2]), preferred_element_type=F32
    ).astype(BF16)

    def core_copy(ch):
        return remote(cs.at[ch], cr.at[ch], c_send.at[ch], c_recv.at[ch], other_c)

    def y_copy(ch):
        return remote(ys.at[ch], yr.at[ch], y_send.at[ch], y_recv.at[ch], other_y)

    def z_copy(ch, zz):
        return remote(
            zs.at[ch, zz], zr.at[ch, z], z_send.at[ch, zz], z_recv.at[ch, z], dev(zz, y, c)
        )

    def z_wait(ch, zz):
        remote(
            zs.at[ch, zz], zr.at[ch, zz], z_send.at[ch, zz], z_recv.at[ch, zz], dev(zz, y, c)
        ).wait_recv()

    def matmul(ch):
        weight_copies[ch].wait()
        step = min(1024, NW)
        for i in range(NW // step):
            off = ch * NW + i * step
            pf[ch, :, i * step : (i + 1) * step] = jnp.dot(
                rows[...], wo[:, off : off + step], preferred_element_type=F32
            )
        cs[ch] = pf[ch, pl.ds(pl.multiple_of((1 - c) * H, H), H), :].astype(BF16)
        core_copy(ch).start()

    def core_step(ch):
        core_copy(ch).wait_recv()
        s1[ch] = pf[ch, pl.ds(pl.multiple_of(c * H, H), H), :] + cr[ch].astype(F32)
        ys[ch] = s1[ch, pl.ds(pl.multiple_of((1 - y) * Q, Q), Q), :].astype(BF16)
        y_copy(ch).start()

    def y_step(ch):
        y_copy(ch).wait_recv()
        s = s1[ch, pl.ds(pl.multiple_of(y * Q, Q), Q), :] + yr[ch].astype(F32)
        for zz in range(Z):
            zf[ch, zz] = s[zz * rl : (zz + 1) * rl]
            zs[ch, zz] = s[zz * rl : (zz + 1) * rl].astype(BF16)
        for k in range(1, Z):
            z_copy(ch, lax.rem(z + k, Z)).start()

    def z_step(ch):
        cols = slice(ch * NW, (ch + 1) * NW)
        total = x_ref[:, cols].astype(F32) + zf[ch, z]
        for k in range(1, Z):
            zz = lax.rem(z + k, Z)
            z_wait(ch, zz)
            total = total + zr[ch, zz].astype(F32)
        out_ref[:, cols] = total.astype(BF16)

    for i in range(NF + 5):
        if i < NF:
            matmul(i)
        if 0 <= i - 1 < NF:
            core_step(i - 1)
        if 0 <= i - 3 < NF:
            y_step(i - 3)
        if 0 <= i - 5 < NF:
            z_step(i - 5)
    for k in range(1, n):
        p = lax.rem(me + k, n)
        remote(att_ref.at[p], ra.at[me], a_send.at[p], a_recv.at[me], p).wait_send()
    for ch in range(NF):
        core_copy(ch).wait_send()
        y_copy(ch).wait_send()
        for k in range(1, Z):
            z_copy(ch, lax.rem(z + k, Z)).wait_send()


def project_out(n, att, ret, x, wo):
    rl, D = x.shape
    NF = 8
    NW = D // NF
    R = n * rl
    Z = n // 4
    vm = pl.BlockSpec(memory_space=pltpu.VMEM)
    hbm = pl.BlockSpec(memory_space=pl.ANY)
    dma = pltpu.SemaphoreType.DMA
    return pl.pallas_call(
        functools.partial(second_kernel, n, NF),
        out_shape=jax.ShapeDtypeStruct((rl, D), BF16),
        in_specs=[vm, vm, vm, hbm],
        out_specs=vm,
        scratch_shapes=[
            pltpu.VMEM(wo.shape, BF16),
            pltpu.VMEM(att.shape, BF16),
            pltpu.VMEM((R, wo.shape[0]), BF16),
            pltpu.VMEM((NF, R, NW), F32),
            pltpu.VMEM((NF, R // 2, NW), BF16),
            pltpu.VMEM((NF, R // 2, NW), BF16),
            pltpu.VMEM((NF, R // 2, NW), F32),
            pltpu.VMEM((NF, R // 4, NW), BF16),
            pltpu.VMEM((NF, R // 4, NW), BF16),
            pltpu.VMEM((NF, Z, rl, NW), F32),
            pltpu.VMEM((NF, Z, rl, NW), BF16),
            pltpu.VMEM((NF, Z, rl, NW), BF16),
            dma((NF,)),
            dma((n,)),
            dma((n,)),
            dma((NF,)),
            dma((NF,)),
            dma((NF,)),
            dma((NF,)),
            dma((NF, Z)),
            dma((NF, Z)),
        ],
        compiler_params=pltpu.CompilerParams(
            collective_id=1, has_side_effects=True, vmem_limit_bytes=60 * 1024 * 1024
        ),
        name="project_out",
    )(att, ret, x, wo)


def attend_slots(probe_vectors, new_kv, keys, values, slot_lengths):
    slots = probe_vectors.shape[0]
    query_heads = probe_vectors.reshape(slots, KV, HEADS // KV, DH)
    key_heads = keys.reshape(slots, CACHE, KV, DH)
    value_heads = values.reshape(slots, CACHE, KV, DH)
    inverse = 1.0 / jnp.sqrt(jnp.float32(DH))
    scores = (
        jnp.einsum("skgd,sjkd->skgj", query_heads, key_heads, preferred_element_type=jnp.float32)
        * inverse
    )
    visible = (jnp.arange(CACHE, dtype=jnp.int32)[None, :] < slot_lengths[:, None])[
        :, None, None, :
    ]
    scores = jnp.where(visible, scores, jnp.float32(-1e30))
    new_keys = new_kv[:, : KV * DH].astype(jnp.float32).reshape(slots, KV, 1, DH)
    new_values = new_kv[:, KV * DH :].astype(jnp.float32).reshape(slots, KV, 1, DH)
    own_score = jnp.sum(query_heads.astype(jnp.float32) * new_keys, axis=-1) * inverse
    highest = jnp.maximum(jnp.max(scores, axis=-1), own_score)
    expo_cache = jnp.where(visible, jnp.exp(scores - highest[..., None]), jnp.float32(0.0))
    expo_new = jnp.exp(own_score - highest)
    denominator = jnp.sum(expo_cache, axis=-1) + expo_new
    weights = (expo_cache / denominator[..., None]).astype(jnp.bfloat16)
    weight_new = (expo_new / denominator).astype(jnp.bfloat16)
    summed = jnp.einsum("skgj,sjkd->skgd", weights, value_heads, preferred_element_type=jnp.float32)
    summed = summed + weight_new.astype(jnp.float32)[..., None] * new_values
    return summed.reshape(slots, HEADS * DH).astype(jnp.bfloat16)


def local(
    remaining_states,
    scaling_factor_vector,
    probe_projection_matrix,
    memory_projection_matrix,
    final_projection_matrix,
    memorized_address_tensor,
    memorized_content_tensor,
    retained_sequence_ids,
    occupied_positions,
):
    n = lax.axis_size("gx")
    me = lax.axis_index("gx")
    slots = memorized_address_tensor.shape[0]
    rl = remaining_states.shape[0]
    R = n * rl
    q_all, kv_all = project_in(
        n,
        remaining_states,
        scaling_factor_vector,
        probe_projection_matrix,
        memory_projection_matrix,
    )
    mine = (
        retained_sequence_ids[None, :]
        == (me * slots + jnp.arange(slots, dtype=jnp.int32))[:, None]
    ).astype(BF16)
    owner_queries = jnp.einsum(
        "sr,drc->sdc", mine, q_all, preferred_element_type=F32
    ).astype(BF16).reshape(slots, -1)
    new_kv = jnp.dot(
        mine, kv_all.reshape(R, -1), preferred_element_type=F32
    ).astype(BF16)
    attended = attend_slots(
        owner_queries,
        new_kv,
        memorized_address_tensor,
        memorized_content_tensor,
        occupied_positions,
    )
    att = jnp.transpose(attended.reshape(slots, n, -1), (1, 0, 2))
    ids = jnp.transpose(
        retained_sequence_ids.reshape(n // 4, 2, 2, rl), (2, 1, 0, 3)
    ).reshape(R)
    ret = (ids[:, None] == jnp.arange(n * slots, dtype=jnp.int32)[None, :]).astype(BF16)
    return project_out(n, att, ret, remaining_states, final_projection_matrix)


def solution(mesh):
    placed = (
        P(("grp", "gx"), None),
        P(),
        P(None, "gx"),
        P("gx", None),
        P("gx", None),
        P(("grp", "gx"), None, None),
        P(("grp", "gx"), None, None),
        P("grp"),
        P(("grp", "gx")),
    )
    return jax.shard_map(
        local, mesh=mesh, in_specs=placed, out_specs=P(("grp", "gx"), None), check_vma=False
    )
```

time: 280 us -> 109 us (0.39)
  waiting for transfers between devices: 194 us -> 0 us
  Pallas kernels: 0 us -> 90.6 us
  matrix products: 34.8 us -> 9.91 us
  blocking collectives: 17.7 us -> 0 us
  between operations: 13.9 us -> 0.14 us
  other arithmetic: 8.92 us -> 2 us
  starting transfers between devices: 3.66 us -> 0 us
    unnamed x4 -> x0, waiting for transfers between devices: 109 us -> none
    pallas_call x0 -> x2, Pallas kernels: none -> 90.6 us  [the longest x1 52.9 us: project_in(): pl.pallas_call(functools.partial(first_kernel, n, NC), out_shape=(jax.Sha...]
    all_gather x1 -> x0, waiting for transfers between devices: 44.3 us -> none  [local(): lax.all_gather(normalize(remaining_states, scaling_factor_vector), 'gx',...]
    reduce_scatter x1 -> x0, waiting for transfers between devices: 26.1 us -> none  [local(): lax.psum_scatter(jnp.dot(sliced, kv_part, precision=lax.Precision.HIGHEST...]
    dot_general x4 -> x2, matrix products: 25.5 us -> 1.78 us  [the longest x1 1.58 us: local(): jnp.einsum('sr,drc->sdc', mine, q_all, preferred_element_type=F32)]
    all_to_all x1 -> x0, blocking collectives: 17.7 us -> none  [local(): lax.all_to_all(attended, 'gx', split_axis=1, concat_axis=0, tiled=True)]
    all_to_all x1 -> x0, waiting for transfers between devices: 14.1 us -> none  [local(): lax.all_to_all(query_slots, 'gx', split_axis=0, concat_axis=1, tiled=True)]
    all_to_all x1 -> x0, starting transfers between devices: 3.57 us -> none  [local(): lax.all_to_all(query_slots, 'gx', split_axis=0, concat_axis=1, tiled=True)]
  transfers between devices with their start and end apart: 4 -> 0, of which waited for: 4 -> 0; matrix products, arithmetic and copies ran while one was open for 6% -> 0% of each run, Pallas kernels for 0% -> 0%
where the time goes in v1:
time: 109 us
  Pallas kernels  90.6 us (83%)
  matrix products  9.91 us (9%)
  local copies, waits for them, and re-layouts  6.22 us (6%)
  other arithmetic  2 us (2%)
    pallas_call x1, Pallas kernels, project_in(): pl.pallas_call(functools.partial(first_kernel, n, NC), out_shape=(jax.Sha...  52.9 us
    pallas_call x1, Pallas kernels, project_out(): pl.pallas_call(functools.partial(second_kernel, n, NF), out_shape=jax.Sha...  37.7 us
    dot_general x1, matrix products, attend_slots(): jnp.einsum('skgd,sjkd->skgj', query_heads, key_heads, preferred_element_t...  4.58 us
    dot_general x1, matrix products, attend_slots(): jnp.einsum('skgj,sjkd->skgd', weights, value_heads, preferred_element_typ...  3.54 us

profile of v1, /device:TPU:0, one launch (start us, length us, event | category | flops | bytes accessed | tf_op | source)
XLA Modules:
  0.0 108.9 jit_solution(181711468425848949)
XLA Ops:
  0.0 1.4 %reshape.67.gain_ref = bf16[1,16384]{1,0:T(2,128)(2,1)} reshape(bf16[16384]{0:T(1024)(128)(2,1)} %param.10) | data formatting | bytes 65536 | tf_op jit(solution)/shard_map/reshape | solution.py:298
  1.4 0.0 copy-start
  1.4 52.9 %project_in.1 = (bf16[1,16,64,512]{3,2,1,0:T(8,128)(2,1)}, bf16[1,16,4,1024]{3,2,1,0:T(4,128)(2,1)}) custom-call(bf16[4,16384]{1,0:T(4,128)(2,1)} %x_ref.3, bf16[1,16384]{1,0:T(2,128)(2,1)} %reshape.67.gain_ref, bf16[16384,512]{1,0:T(8,128)(2,1)} %wq_hbm.1, bf16[1024,1024]{1,0:T(8,128)(2,1)} %wkv_hbm.1), custom_call_target="tpu_custom_call" | custom-call | tf_op jit(solution)/shard_map/project_in/pallas_call | solution.py:267
  54.3 0.0 copy-start.1
  54.3 0.0 copy-done
  54.4 1.6 %convolution_convert_fusion = bf16[32,16,512]{2,0,1:T(8,128)(2,1)S(1)} fusion(bf16[1,16,64,512]{3,2,1,0:T(8,128)(2,1)} %get-tuple-element.7, s32[64]{0:T(128)S(1)} %copy-done, s32[32]{0:T(128)S(1)} %iota_add_fusion), kind=kOutput, calls=%fused_computation.9 | convolution fusion | flops 33818624 | bytes 1573248 | tf_op jit(solution)/shard_map/sr,drc->sdc/dot_general | solution.py:501
  55.9 0.3 copy.13
  56.2 0.3 reshape_reshape.3
  56.6 0.9 reshape_squeeze.3
  57.5 0.2 convolution_convert_fusion.1
  57.8 0.4 multiply_reduce_fusion
  58.2 0.0 copy-done.1
  58.2 0.1 iota_compare_fusion.1
  58.3 4.6 %fusion.33 = (f32[32,4,16]{2,1,0:T(4,128)S(1)}, f32[32,4,16,128]{3,2,1,0:T(8,128)S(1)}) fusion(bf16[32,4,16,128]{3,2,1,0:T(8,128)(2,1)S(1)} %reshape_reshape.3, pred[32,128]{1,0:T(8,128)(4,1)S(1)} %iota_compare_fusion.1, bf16[32,128,512]{2,1,0:T(8,128)(2,1)} %param.14), kind=kOutput, calls=%fused_computation.40 | convolution fusion | flops 67893248 | bytes 5779456 | tf_op jit(solution)/shard_map/skgd,sjkd->skgj/dot_general | solution.py:453
  62.9 0.7 fusion.19
  63.6 0.1 fusion.27
  63.7 3.5 %fusion.15 = bf16[32,4,16,128]{3,2,1,0:T(8,128)(2,1)S(1)} fusion(f32[32,4,16,128]{3,2,1,0:T(8,128)S(1)} %get-tuple-element.14, f32[32,4,128]{2,1,0:T(4,128)S(1)} %reshape.72, f32[32,4,16]{2,1,0:T(4,128)S(1)} %get-tuple-element.10, f32[32,4,16]{2,1,0:T(4,128)S(1)} %get-tuple-element.9, f32[32,4,16]{2,1,0:T(4,128)S(1)} %multiply_maximum_fusion, ...), kind=kOutput, calls=%fused_computation.10 | convolution fusion | flops 68943872 | bytes 5861376 | tf_op jit(solution)/shard_map/skgj,sjkd->skgd/dot_general | solution.py:469
  67.2 0.3 convert_element_type.46
  67.5 1.1 copy.39
  68.6 0.1 reshape.70
  68.7 0.1 eq.31
  68.8 0.7 fusion.24.ret_ref
  69.6 37.7 %project_out.1 = bf16[4,16384]{1,0:T(4,128)(2,1)} custom-call(bf16[16,32,512]{2,1,0:T(8,128)(2,1)} %bitcast.38, bf16[64,512]{1,0:T(8,128)(2,1)} %fusion.24.ret_ref, bf16[4,16384]{1,0:T(4,128)(2,1)} %x_ref.3, bf16[512,16384]{1,0:T(8,128)(2,1)} %wo_hbm.1), custom_call_target="tpu_custom_call" | custom-call | tf_op jit(solution)/shard_map/project_out/pallas_call | solution.py:411
  107.3 1.6 %copy.41 = bf16[4,16384]{1,0:T(4,128)(2,1)} copy(bf16[4,16384]{1,0:T(4,128)(2,1)} %project_out.1) | data formatting | bytes 262144
  (6 shorter events, 0.1 us)
Async XLA Ops:
  1.4 52.9 %copy-start = (s32[64]{0:T(128)S(1)}, s32[64]{0:T(128)}, u32[]{:S(2)}) copy-start(s32[64]{0:T(128)} %param.16) | copy-start | bytes 772
  54.3 3.9 %copy-start.1 = (s32[32]{0:T(128)S(1)}, s32[32]{0:T(128)}, u32[]{:S(2)}) copy-start(s32[32]{0:T(128)} %param.17) | copy-start | bytes 388

commit v2 on v1

--- a/solution.py
+++ b/solution.py
@@ -256,7 +256,7 @@
 
 def project_in(n, x, gain, wq, wkv):
     rl, D = x.shape
-    NC = 4
+    NC = 2
     CW = D // NC
     cols = wq.shape[1]
     wide = wkv.shape[1]
@@ -401,7 +401,7 @@
 
 def project_out(n, att, ret, x, wo):
     rl, D = x.shape
-    NF = 8
+    NF = 4
     NW = D // NF
     R = n * rl
     Z = n // 4

time: 109 us -> 104 us (0.954)
  Pallas kernels: 90.6 us -> 85.8 us
    pallas_call x1, Pallas kernels: 52.9 us -> 47.7 us  [project_in(): pl.pallas_call(functools.partial(first_kernel, n, NC), out_shape=(jax.Sha...]
where the time goes in v2:
time: 104 us
  Pallas kernels  85.8 us (82%)
  matrix products  9.91 us (10%)
  local copies, waits for them, and re-layouts  6.22 us (6%)
  other arithmetic  2 us (2%)
    pallas_call x1, Pallas kernels, project_in(): pl.pallas_call(functools.partial(first_kernel, n, NC), out_shape=(jax.Sha...  47.7 us
    pallas_call x1, Pallas kernels, project_out(): pl.pallas_call(functools.partial(second_kernel, n, NF), out_shape=jax.Sha...  38 us
    dot_general x1, matrix products, attend_slots(): jnp.einsum('skgd,sjkd->skgj', query_heads, key_heads, preferred_element_t...  4.58 us
    dot_general x1, matrix products, attend_slots(): jnp.einsum('skgj,sjkd->skgd', weights, value_heads, preferred_element_typ...  3.54 us

profile of v2, /device:TPU:0, one launch (start us, length us, event | category | flops | bytes accessed | tf_op | source)
XLA Modules:
  0.0 104.0 jit_solution(15210440863973421372)
XLA Ops:
  0.0 1.4 %reshape.67.gain_ref = bf16[1,16384]{1,0:T(2,128)(2,1)} reshape(bf16[16384]{0:T(1024)(128)(2,1)} %param.10) | data formatting | bytes 65536 | tf_op jit(solution)/shard_map/reshape | solution.py:298
  1.4 0.0 copy-start
  1.4 47.7 %project_in.1 = (bf16[1,16,64,512]{3,2,1,0:T(8,128)(2,1)}, bf16[1,16,4,1024]{3,2,1,0:T(4,128)(2,1)}) custom-call(bf16[4,16384]{1,0:T(4,128)(2,1)} %x_ref.3, bf16[1,16384]{1,0:T(2,128)(2,1)} %reshape.67.gain_ref, bf16[16384,512]{1,0:T(8,128)(2,1)} %wq_hbm.1, bf16[1024,1024]{1,0:T(8,128)(2,1)} %wkv_hbm.1), custom_call_target="tpu_custom_call" | custom-call | tf_op jit(solution)/shard_map/project_in/pallas_call | solution.py:267
  49.2 0.0 copy-start.1
  49.2 0.0 copy-done
  49.2 1.6 %convolution_convert_fusion = bf16[32,16,512]{2,0,1:T(8,128)(2,1)S(1)} fusion(bf16[1,16,64,512]{3,2,1,0:T(8,128)(2,1)} %get-tuple-element.7, s32[64]{0:T(128)S(1)} %copy-done, s32[32]{0:T(128)S(1)} %iota_add_fusion), kind=kOutput, calls=%fused_computation.9 | convolution fusion | flops 33818624 | bytes 1573248 | tf_op jit(solution)/shard_map/sr,drc->sdc/dot_general | solution.py:501
  50.8 0.3 copy.13
  51.1 0.3 reshape_reshape.3
  51.4 0.9 reshape_squeeze.3
  52.4 0.2 convolution_convert_fusion.1
  52.6 0.4 multiply_reduce_fusion
  53.0 0.0 copy-done.1
  53.0 0.1 iota_compare_fusion.1
  53.1 4.6 %fusion.33 = (f32[32,4,16]{2,1,0:T(4,128)S(1)}, f32[32,4,16,128]{3,2,1,0:T(8,128)S(1)}) fusion(bf16[32,4,16,128]{3,2,1,0:T(8,128)(2,1)S(1)} %reshape_reshape.3, pred[32,128]{1,0:T(8,128)(4,1)S(1)} %iota_compare_fusion.1, bf16[32,128,512]{2,1,0:T(8,128)(2,1)} %param.14), kind=kOutput, calls=%fused_computation.40 | convolution fusion | flops 67893248 | bytes 5779456 | tf_op jit(solution)/shard_map/skgd,sjkd->skgj/dot_general | solution.py:453
  57.7 0.7 fusion.19
  58.4 0.1 fusion.27
  58.5 3.5 %fusion.15 = bf16[32,4,16,128]{3,2,1,0:T(8,128)(2,1)S(1)} fusion(f32[32,4,16,128]{3,2,1,0:T(8,128)S(1)} %get-tuple-element.14, f32[32,4,128]{2,1,0:T(4,128)S(1)} %reshape.72, f32[32,4,16]{2,1,0:T(4,128)S(1)} %get-tuple-element.10, f32[32,4,16]{2,1,0:T(4,128)S(1)} %get-tuple-element.9, f32[32,4,16]{2,1,0:T(4,128)S(1)} %multiply_maximum_fusion, ...), kind=kOutput, calls=%fused_computation.10 | convolution fusion | flops 68943872 | bytes 5861376 | tf_op jit(solution)/shard_map/skgj,sjkd->skgd/dot_general | solution.py:469
  62.1 0.3 convert_element_type.46
  62.4 1.1 %copy.39 = bf16[32,16,512]{2,0,1:T(8,128)(2,1)} copy(bf16[32,16,512]{2,1,0:T(8,128)(2,1)S(1)} %convert_element_type.46) | data formatting | bytes 1048576 | tf_op jit(solution)/shard_map/convert_element_type | solution.py:471
  63.5 0.1 reshape.70
  63.6 0.1 eq.31
  63.7 0.7 fusion.24.ret_ref
  64.4 38.0 %project_out.1 = bf16[4,16384]{1,0:T(4,128)(2,1)} custom-call(bf16[16,32,512]{2,1,0:T(8,128)(2,1)} %bitcast.38, bf16[64,512]{1,0:T(8,128)(2,1)} %fusion.24.ret_ref, bf16[4,16384]{1,0:T(4,128)(2,1)} %x_ref.3, bf16[512,16384]{1,0:T(8,128)(2,1)} %wo_hbm.1), custom_call_target="tpu_custom_call" | custom-call | tf_op jit(solution)/shard_map/project_out/pallas_call | solution.py:411
  102.4 1.6 %copy.41 = bf16[4,16384]{1,0:T(4,128)(2,1)} copy(bf16[4,16384]{1,0:T(4,128)(2,1)} %project_out.1) | data formatting | bytes 262144
  (6 shorter events, 0.1 us)
Async XLA Ops:
  1.4 47.8 %copy-start = (s32[64]{0:T(128)S(1)}, s32[64]{0:T(128)}, u32[]{:S(2)}) copy-start(s32[64]{0:T(128)} %param.16) | copy-start | bytes 772
  49.2 3.9 %copy-start.1 = (s32[32]{0:T(128)S(1)}, s32[32]{0:T(128)}, u32[]{:S(2)}) copy-start(s32[32]{0:T(128)} %param.17) | copy-start | bytes 388
